TPU v7x, 256 devices: a whole 4x4x8 slice. The times are simulated.
256 devices in a mesh: grid: 32 (over y, x, core), rows: 8 (over z).
Axes of the slice: x: 4, y: 4, z: 8, core: 2. Of those that a mesh axis runs over, the one named last changes fastest.
Arguments:
- density: bfloat16 [32, 128, 4096], P(None, 'rows', 'grid'), as said below
- basis_values: bfloat16 [64, 16, 128, 512], P('grid', None, 'rows'), may hold values from -0.59765625 to 0.59765625
- grid_points: float32 [64, 3, 512], P('grid'), may hold values from -4 to 4
- grid_weights: float32 [64, 512], P('grid'), may hold values from 0.05 to 1
- screened_blocks: int32 [64, 16], P('grid'), may hold values from 0 to 31, as said below
Outputs:
- exchange: float32 [32, 128, 4096], P(None, 'rows', 'grid')
Inputs may be any that keep to these rules, and one draw needn't show every extreme that they name: density is symmetric: density[a, i, b * 128 + j] equals density[b, j, a * 128 + i]. `screened_blocks`: each row holds 16 distinct block numbers.
All inputs are finite; a program needn't handle non-finite values.
Results may differ from a plain program's by a relative error of at most 0.00055.
The roundings to bfloat16 on the way count: a program that leaves them out, or rounds other values in their place, can miss the bound.
Values may be sent and summed in bfloat16 or wider, within the bound.
A program may use at most 64 MiB of HBM per device.

v0:
```python
import jax
import jax.numpy as jnp
from jax import lax
from jax.sharding import PartitionSpec as P


def copy_for_each(shard, axis):
    copies = jnp.broadcast_to(shard, (lax.axis_size(axis), *shard.shape))
    return lax.all_to_all(copies, axis, split_axis=0, concat_axis=0, tiled=True)


def joined_along(blocks, dim):
    shape = list(blocks.shape[1:])
    shape[dim] *= blocks.shape[0]
    return jnp.moveaxis(blocks, 0, dim).reshape(shape)


def gather_directly(shard, axis, dim):
    blocks = copy_for_each(shard, axis)
    return joined_along(blocks, dim)


def body(density, basis_values, grid_points, grid_weights, screened_blocks):
    nblocks = density.shape[0]
    rows_mine = density.shape[1]
    block_size = rows_mine * lax.axis_size("rows")
    nbasis = nblocks * block_size
    nsig = basis_values.shape[1]
    npoints = basis_values.shape[3]
    stripe = lax.all_gather(density, "grid", axis=2, tiled=True)
    totals = jnp.zeros((nblocks, rows_mine, nblocks, block_size), jnp.float32)
    for batch_index in range(basis_values.shape[0]):
        blocks = screened_blocks[batch_index]
        row_pick = jnp.take(stripe, blocks, axis=0).reshape(nsig * rows_mine, nblocks, block_size)
        chosen = jnp.take(row_pick, blocks, axis=1)
        local_values = basis_values[batch_index]
        x_mine = local_values.reshape(nsig * rows_mine, npoints)
        fsum = jnp.einsum(
            "mtk,tkp->mp",
            chosen,
            gather_directly(local_values, "rows", 1),
            preferred_element_type=jnp.float32,
        )
        fmat = fsum.astype(jnp.bfloat16)
        intersection_part = lax.dot_general(
            x_mine, fmat, (((0,), (0,)), ((), ())), preferred_element_type=jnp.float32
        )
        intersection = lax.psum(intersection_part, "rows")
        places = grid_points[batch_index]
        weights = grid_weights[batch_index]
        diffs = places[:, :, None] - places[:, None, :]
        kern = 1.0 / jnp.sqrt(jnp.sum(diffs * diffs, axis=0) + 0.5)
        mixed = (weights[:, None] * kern * intersection).astype(jnp.bfloat16)
        potential = (
            jnp.dot(x_mine, mixed, preferred_element_type=jnp.float32) * weights[None, :]
        ).astype(jnp.bfloat16)
        potential = potential.reshape(nsig, rows_mine, npoints)
        block_k = jnp.einsum(
            "mp,tkp->mtk",
            x_mine,
            lax.all_gather(potential, "rows", axis=1, tiled=True),
            preferred_element_type=jnp.float32,
        )
        block_k = block_k.reshape(nsig, rows_mine, nsig, block_size)
        totals = totals.at[blocks[:, None], :, blocks[None, :], :].add(
            block_k.transpose(0, 2, 1, 3)
        )
    return lax.psum_scatter(
        totals.reshape(nblocks, rows_mine, nbasis), "grid", scatter_dimension=2, tiled=True
    )


def solution(mesh):
    placed = (
        P(None, "rows", "grid"),
        P("grid", None, "rows", None),
        P("grid", None, None),
        P("grid", None),
        P("grid", None),
    )
    return jax.shard_map(
        body, mesh=mesh, in_specs=placed, out_specs=P(None, "rows", "grid"), check_vma=False
    )
```

profile of v0, /device:TPU:2, one launch (start us, length us, event | category | flops | bytes accessed | tf_op | source)
XLA Modules:
  0.0 494.6 jit_solution(1196830963108560420)
XLA Ops:
  6.5 0.7 all-gather.4.cloned.1.call-update
  7.3 1.1 slice_bitcast_fusion
  8.4 0.3 broadcast_in_dim.59
  8.6 59.6 %all_to_all.10 = bf16[8,16,16,512]{3,2,1,0:T(8,128)(2,1)} all-to-all(bf16[8,16,16,512]{3,2,1,0:T(8,128)(2,1)S(1)} %broadcast_in_dim.59), channel_id=1, replica_groups=mesh['grid'=32,'rows'=8] {'rows'}, dimensions={0} | all-to-all | bytes 4194304 | tf_op jit(solution)/shard_map/all_to_all | solution.py:9
  68.2 1.6 broadcast_in_dim.55
  69.8 3.7 all-to-all-start
  73.5 0.0 all-reduce.3.cloned.1.call-start
  73.7 3.2 copy.34
  76.8 46.5 %all-to-all-done = bf16[8,16,16,512]{3,2,1,0:T(8,128)(2,1)S(1)} async-done(((bf16[8,16,16,512]{3,2,1,0:T(8,128)(2,1)}), bf16[8,16,16,512]{3,2,1,0:T(8,128)(2,1)S(1)}, u32[]{:S(2)}, u32[]{:S(2)}) %all-to-all-start) | async-done | bytes 2097184 | tf_op jit(solution)/shard_map/all_to_all | solution.py:9
  123.3 1.6 copy.29
  124.9 2.9 gather_fusion.2
  127.8 0.3 broadcast_select_fusion
  128.0 0.5 copy.42
  128.5 0.8 copy.33
  129.3 1.7 gather_fusion.3
  131.1 2.9 gather_fusion
  134.0 0.3 broadcast_select_fusion.1
  134.2 0.5 copy.41
  134.7 0.8 copy.28
  135.5 1.7 gather_fusion.1
  137.2 4.1 convolution_bitcast_fusion.2
  141.3 3.3 convolution_bitcast_fusion.3
  144.6 0.6 copy-done.1
  145.3 0.4 multiply_reduce_fusion.1
  145.7 0.3 copy.27
  146.0 77.3 %all-reduce.3.cloned.1.call-done = (f32[512,512]{0,1:T(8,128)}, f32[512,512]{0,1:T(8,128)}) async-done(((f32[512,512]{0,1:T(8,128)}, f32[512,512]{0,1:T(8,128)}), (f32[512,512]{0,1:T(8,128)}, f32[512,512]{0,1:T(8,128)})) %all-reduce.3.cloned.1.call-update) | async-done | bytes 2097168 | tf_op jit(solution)/shard_map/psum | solution.py:48
  223.3 2.3 fusion
  225.7 0.0 all-gather.8.cloned.1.call-start
  225.7 0.4 multiply_reduce_fusion
  226.1 0.3 copy.32
  226.4 2.3 fusion.1
  228.7 0.2 reduce-scatter.2.cloned.1.call-start
  229.0 0.1 or_select_fusion
  229.1 0.1 reshape.140
  229.2 0.1 reshape.146
  229.3 36.4 %all-gather.6.cloned.1.call-done = bf16[16,128,512]{2,1,0:T(8,128)(2,1)} async-done(((bf16[16,16,512]{2,1,0:T(8,128)(2,1)}), bf16[16,128,512]{2,1,0:T(8,128)(2,1)}) %all-gather.6.cloned.1.call-update) | async-done | bytes 2097168 | tf_op jit(solution)/shard_map/all_gather | solution.py:61
  265.7 2.3 convolution_bitcast_fusion.1
  268.0 2.0 copy.30
  270.0 2.3 copy.31
  272.2 34.5 %all-gather.8.cloned.1.call-done = bf16[16,128,512]{2,1,0:T(8,128)(2,1)} async-done(((bf16[16,16,512]{2,1,0:T(8,128)(2,1)}), bf16[16,128,512]{2,1,0:T(8,128)(2,1)}) %all-gather.8.cloned.1.call-update) | async-done | bytes 2097168 | tf_op jit(solution)/shard_map/all_gather | solution.py:61
  306.8 3.6 convolution_bitcast_fusion
  310.4 3.1 copy.35
  313.5 3.6 copy.36
  317.1 4.2 broadcast_in_dim.51
  321.3 28.4 %scatter_fusion = f32[32,16,32,128]{3,1,2,0:T(8,128)} fusion(f32[32,16,32,128]{3,1,2,0:T(8,128)} %broadcast_in_dim.51, s32[256]{0:T(256)S(1)} %reshape.140, f32[256,16,128]{2,1,0:T(8,128)S(1)} %bitcast.107), kind=kCustom, calls=%fused_computation.4 | custom fusion | flops 524288 | bytes 6293504 | tf_op jit(solution)/shard_map/scatter-add | solution.py:65
  349.7 31.8 %scatter_fusion.1 = f32[32,16,32,128]{3,1,2,0:T(8,128)} fusion(f32[32,16,32,128]{3,1,2,0:T(8,128)} %scatter_fusion, s32[256]{0:T(256)S(1)} %reshape.146, f32[256,16,128]{2,1,0:T(8,128)} %bitcast.108), kind=kCustom, calls=%fused_computation.5 | custom fusion | flops 524288 | bytes 6293504 | tf_op jit(solution)/shard_map/scatter-add | solution.py:65
  381.5 7.8 %copy_bitcast_fusion = f32[32,16,4096]{2,1,0:T(8,128)} fusion(f32[32,16,32,128]{3,1,2,0:T(8,128)} %scatter_fusion.1), kind=kLoop, calls=%fused_computation.6 | loop fusion | bytes 16777216 | tf_op jit(solution)/shard_map/reshape | solution.py:69
  389.3 98.8 %reduce-scatter.2.cloned.1.call-done = f32[32,16,128]{2,1,0:T(8,128)} async-done(((f32[32,16,4096]{2,1,0:T(8,128)}), f32[32,16,128]{2,1,0:T(8,128)}) %reduce-scatter.2.cloned.1.call-update) | async-done | bytes 262160 | tf_op jit(solution)/shard_map/reduce_scatter | solution.py:68
  (25 shorter events, 0.2 us)
Async XLA Ops:
  6.5 118.4 %all-gather.4.cloned.1.call-start = ((), (), s32[]{:S(2)}) async-start(), calls=%async_computation.3 | async-start | bytes 4325376 | tf_op jit(solution)/shard_map/all_gather | solution.py:30
  69.8 3.8 copy-start.3
  69.8 53.5 %all-to-all-start = ((bf16[8,16,16,512]{3,2,1,0:T(8,128)(2,1)}), bf16[8,16,16,512]{3,2,1,0:T(8,128)(2,1)S(1)}, u32[]{:S(2)}, u32[]{:S(2)}) async-start(bf16[8,16,16,512]{3,2,1,0:T(8,128)(2,1)} %broadcast_in_dim.55), calls=%async_computation | async-start | bytes 4194304 | tf_op jit(solution)/shard_map/all_to_all | solution.py:9
  73.5 149.8 %all-reduce.3.cloned.1.call-start = ((), (), s32[]{:S(2)}) async-start(), calls=%async_computation.7 | async-start | bytes 4194304 | tf_op jit(solution)/shard_map/psum | solution.py:48
  137.2 4.1 copy-start
  144.6 0.7 copy-start.1
  144.6 1.4 copy-start.2
  144.6 121.1 %all-gather.6.cloned.1.call-start = ((), (), s32[]{:S(2)}) async-start(), calls=%async_computation.4 | async-start | bytes 2359296 | tf_op jit(solution)/shard_map/all_gather | solution.py:61
  225.7 81.1 %all-gather.8.cloned.1.call-start = ((), (), s32[]{:S(2)}) async-start(), calls=%async_computation.5 | async-start | bytes 2359296 | tf_op jit(solution)/shard_map/all_gather | solution.py:61
  228.7 259.3 %reduce-scatter.2.cloned.1.call-start = ((), (), s32[]{:S(2)}) async-start(), calls=%async_computation.6 | async-start | bytes 8650752 | tf_op jit(solution)/shard_map/reduce_scatter | solution.py:68
Sparse Core Ops, SparseCore 0:
  9.8 56.2 all-gather.3
  144.7 78.5 all-reduce.2
  225.8 39.8 all-gather.5
  267.3 39.4 all-gather.7
  389.4 98.5 reduce-scatter.1
where the time goes:
time: 496 us; the launch traced here: 495 us
  waiting for transfers between devices  294 us (59%)
  other arithmetic  61.6 us (12%)
  blocking collectives  59.6 us (12%)
  local copies, waits for them, and re-layouts  43.8 us (9%)
  matrix products  17.9 us (4%)
  between operations  13.4 us (3%)
    reduce_scatter x1, waiting for transfers between devices, body(): lax.psum_scatter(totals.reshape(nblocks, rows_mine, nbasis), 'grid', scat...  98.8 us
    psum x1, waiting for transfers between devices, body(): intersection = lax.psum(intersection_part, 'rows')  77.3 us
    all_gather x2, waiting for transfers between devices, body(): lax.all_gather(potential, 'rows', axis=1, tiled=True)  70.9 us
    scatter-add x2, other arithmetic, body(): totals.at[blocks[:, None], :, blocks[None, :], :]  60.2 us
    all_to_all x1, blocking collectives, copy_for_each(): return lax.all_to_all(copies, axis, split_axis=0, concat_axis=0, tiled=True)  59.6 us
    all_to_all x1, waiting for transfers between devices, copy_for_each(): return lax.all_to_all(copies, axis, split_axis=0, concat_axis=0, tiled=True)  46.5 us
  transfers between devices with their start and end apart: 6, of which 5 were waited for; matrix products, arithmetic and copies ran while one was open for 4% of the time, Pallas kernels for 0%

commit v1 on v0

--- a/solution.py
+++ b/solution.py
@@ -45,7 +45,8 @@
         intersection_part = lax.dot_general(
             x_mine, fmat, (((0,), (0,)), ((), ())), preferred_element_type=jnp.float32
         )
-        intersection = lax.psum(intersection_part, "rows")
+        shards = lax.all_gather(intersection_part, "rows", axis=0, tiled=False)
+        intersection = shards.sum(axis=0)
         places = grid_points[batch_index]
         weights = grid_weights[batch_index]
         diffs = places[:, :, None] - places[:, None, :]

time: 496 us -> 587 us (1.18)
  waiting for transfers between devices: 294 us -> 404 us
  blocking collectives: 59.6 us -> 0 us
  local copies, waits for them, and re-layouts: 43.8 us -> 65 us
  starting transfers between devices: 4.08 us -> 13.3 us
  other arithmetic: 61.6 us -> 67.7 us
    all_gather x0 -> x2, waiting for transfers between devices: none -> 120 us  [body(): shards = lax.all_gather(intersection_part, 'rows', axis=0, tiled=False)]
    all_to_all x1 -> x2, waiting for transfers between devices: 46.5 us -> 125 us  [copy_for_each(): return lax.all_to_all(copies, axis, split_axis=0, concat_axis=0, tiled=True)]
    psum x1 -> x0, waiting for transfers between devices: 77.3 us -> none  [body(): intersection = lax.psum(intersection_part, 'rows')]
    all_to_all x1 -> x0, blocking collectives: 59.6 us -> none  [copy_for_each(): return lax.all_to_all(copies, axis, split_axis=0, concat_axis=0, tiled=True)]
    unnamed x11 -> x13, local copies, waits for them, and re-layouts: 1.59 us -> 23.9 us
    all_gather x2, waiting for transfers between devices: 70.9 us -> 59.1 us  [body(): lax.all_gather(potential, 'rows', axis=1, tiled=True)]
    all_to_all x1 -> x2, starting transfers between devices: 3.73 us -> 12.2 us  [copy_for_each(): return lax.all_to_all(copies, axis, split_axis=0, concat_axis=0, tiled=True)]
    reduce_sum x0 -> x2, other arithmetic: none -> 6.11 us  [body(): intersection = shards.sum(axis=0)]
  transfers between devices with their start and end apart: 6 -> 8, of which waited for: 5 -> 7; matrix products, arithmetic and copies ran while one was open for 4% -> 10% of each run, Pallas kernels for 0% -> 0%
where the time goes in v1:
time: 587 us; the launch traced here: 580 us
  waiting for transfers between devices  404 us (69%)
  other arithmetic  67.7 us (12%)
  local copies, waits for them, and re-layouts  65 us (11%)
  matrix products  16.8 us (3%)
  between operations  14 us (2%)
  starting transfers between devices  13.3 us (2%)
    all_to_all x2, waiting for transfers between devices, copy_for_each(): return lax.all_to_all(copies, axis, split_axis=0, concat_axis=0, tiled=True)  125 us
    all_gather x2, waiting for transfers between devices, body(): shards = lax.all_gather(intersection_part, 'rows', axis=0, tiled=False)  120 us
    reduce_scatter x1, waiting for transfers between devices, body(): lax.psum_scatter(totals.reshape(nblocks, rows_mine, nbasis), 'grid', scat...  98.8 us
    scatter-add x2, other arithmetic, body(): totals.at[blocks[:, None], :, blocks[None, :], :]  60.2 us
    all_gather x2, waiting for transfers between devices, body(): lax.all_gather(potential, 'rows', axis=1, tiled=True)  59.1 us
    unnamed x13, local copies, waits for them, and re-layouts  23.9 us
    all_to_all x2, starting transfers between devices, copy_for_each(): return lax.all_to_all(copies, axis, split_axis=0, concat_axis=0, tiled=True)  12.2 us
  transfers between devices with their start and end apart: 8, of which 7 were waited for; matrix products, arithmetic and copies ran while one was open for 10% of the time, Pallas kernels for 0%

profile of v1, /device:TPU:2, one launch (start us, length us, event | category | flops | bytes accessed | tf_op | source)
XLA Modules:
  0.0 580.4 jit_solution(16691935981800096354)
XLA Ops:
  6.5 0.7 all-gather.8.cloned.1.call-update
  7.3 1.2 slice_bitcast_fusion
  8.4 1.6 broadcast_in_dim.59
  10.0 8.6 %all-to-all-start.1 = ((bf16[8,16,16,512]{3,2,1,0:T(8,128)(2,1)}), bf16[8,16,16,512]{3,2,1,0:T(8,128)(2,1)S(1)}, u32[]{:S(2)}, u32[]{:S(2)}) async-start(bf16[8,16,16,512]{3,2,1,0:T(8,128)(2,1)} %broadcast_in_dim.59), calls=%async_computation.1 | async-start | bytes 4194304 | tf_op jit(solution)/shard_map/all_to_all | solution.py:9
  18.7 51.1 %all-to-all-done.1 = bf16[8,16,16,512]{3,2,1,0:T(8,128)(2,1)S(1)} async-done(((bf16[8,16,16,512]{3,2,1,0:T(8,128)(2,1)}), bf16[8,16,16,512]{3,2,1,0:T(8,128)(2,1)S(1)}, u32[]{:S(2)}, u32[]{:S(2)}) %all-to-all-start.1) | async-done | bytes 2097184 | tf_op jit(solution)/shard_map/all_to_all | solution.py:9
  69.8 1.6 copy.33
  71.4 2.9 gather_fusion.2
  74.3 0.3 broadcast_select_fusion
  74.6 0.5 copy.43
  75.0 0.8 copy.32
  75.9 1.7 gather_fusion.3
  77.6 4.0 convolution_bitcast_fusion.2
  81.6 1.6 broadcast_in_dim.55
  83.2 3.6 all-to-all-start
  86.8 73.9 %all-to-all-done = bf16[8,16,16,512]{3,2,1,0:T(8,128)(2,1)S(1)} async-done(((bf16[8,16,16,512]{3,2,1,0:T(8,128)(2,1)}), bf16[8,16,16,512]{3,2,1,0:T(8,128)(2,1)S(1)}, u32[]{:S(2)}, u32[]{:S(2)}) %all-to-all-start) | async-done | bytes 2097184 | tf_op jit(solution)/shard_map/all_to_all | solution.py:9
  160.8 1.6 copy.28
  162.3 2.9 gather_fusion
  165.2 0.3 broadcast_select_fusion.1
  165.5 0.5 copy.41
  166.0 0.8 copy.27
  166.8 0.7 gather_fusion.1
  167.6 3.7 convolution_bitcast_fusion.3
  171.3 0.5 all-gather.12.cloned.1.call-start
  171.9 0.4 multiply_reduce_fusion
  172.2 42.7 %all-gather.16.cloned.1.call-done = f32[4096,512]{0,1:T(8,128)} async-done(((f32[512,512]{0,1:T(8,128)}), f32[4096,512]{0,1:T(8,128)}) %all-gather.16.cloned.1.call-update) | async-done | bytes 8388624 | tf_op jit(solution)/shard_map/all_gather | solution.py:48
  214.9 11.5 %copy.44 = f32[64,8,8,512]{3,2,1,0:T(8,128)S(1)} copy(f32[64,8,8,512]{3,1,2,0:T(8,128)} %bitcast.119) | data formatting | bytes 16777216
  226.4 3.1 bitcast_reduce_fusion
  229.5 0.3 copy.34
  229.8 2.1 fusion.1
  232.1 0.4 multiply_reduce_fusion.1
  232.5 77.3 %all-gather.14.cloned.1.call-done = f32[4096,512]{0,1:T(8,128)} async-done(((f32[512,512]{0,1:T(8,128)}), f32[4096,512]{0,1:T(8,128)}) %all-gather.14.cloned.1.call-update) | async-done | bytes 8388624 | tf_op jit(solution)/shard_map/all_gather | solution.py:48
  309.8 11.5 %copy.42 = f32[64,8,8,512]{3,2,1,0:T(8,128)S(1)} copy(f32[64,8,8,512]{3,1,2,0:T(8,128)} %bitcast.120) | data formatting | bytes 16777216
  321.3 3.1 bitcast_reduce_fusion.1
  324.4 0.3 copy.29
  324.7 1.1 fusion
  326.4 24.8 %all-gather.12.cloned.1.call-done = bf16[16,128,512]{2,1,0:T(8,128)(2,1)} async-done(((bf16[16,16,512]{2,1,0:T(8,128)(2,1)}), bf16[16,128,512]{2,1,0:T(8,128)(2,1)}) %all-gather.12.cloned.1.call-update) | async-done | bytes 2097168 | tf_op jit(solution)/shard_map/all_gather | solution.py:62
  351.2 2.3 convolution_bitcast_fusion
  353.6 2.0 copy.35
  355.6 2.3 copy.36
  357.8 34.3 %all-gather.10.cloned.1.call-done = bf16[16,128,512]{2,1,0:T(8,128)(2,1)} async-done(((bf16[16,16,512]{2,1,0:T(8,128)(2,1)}), bf16[16,128,512]{2,1,0:T(8,128)(2,1)}) %all-gather.10.cloned.1.call-update) | async-done | bytes 2097168 | tf_op jit(solution)/shard_map/all_gather | solution.py:62
  392.1 3.6 convolution_bitcast_fusion.1
  395.7 3.1 copy.30
  398.8 3.6 copy.31
  402.4 4.2 broadcast_in_dim.51
  406.6 31.8 %scatter_fusion = f32[32,16,32,128]{3,1,2,0:T(8,128)} fusion(f32[32,16,32,128]{3,1,2,0:T(8,128)} %broadcast_in_dim.51, s32[256]{0:T(256)S(1)} %reshape.140, f32[256,16,128]{2,1,0:T(8,128)} %bitcast.118), kind=kCustom, calls=%fused_computation.4 | custom fusion | flops 524288 | bytes 6293504 | tf_op jit(solution)/shard_map/scatter-add | solution.py:66
  438.4 28.4 %scatter_fusion.1 = f32[32,16,32,128]{3,1,2,0:T(8,128)} fusion(f32[32,16,32,128]{3,1,2,0:T(8,128)} %scatter_fusion, s32[256]{0:T(256)S(1)} %reshape.146, f32[256,16,128]{2,1,0:T(8,128)S(1)} %bitcast.117), kind=kCustom, calls=%fused_computation.5 | custom fusion | flops 524288 | bytes 6293504 | tf_op jit(solution)/shard_map/scatter-add | solution.py:66
  466.8 7.8 %copy_bitcast_fusion = f32[32,16,4096]{2,1,0:T(8,128)} fusion(f32[32,16,32,128]{3,1,2,0:T(8,128)} %scatter_fusion.1), kind=kLoop, calls=%fused_computation.8 | loop fusion | bytes 16777216 | tf_op jit(solution)/shard_map/reshape | solution.py:70
  474.6 98.8 %reduce-scatter.2.cloned.1.call-done = f32[32,16,128]{2,1,0:T(8,128)} async-done(((f32[32,16,4096]{2,1,0:T(8,128)}), f32[32,16,128]{2,1,0:T(8,128)}) %reduce-scatter.2.cloned.1.call-update) | async-done | bytes 262160 | tf_op jit(solution)/shard_map/reduce_scatter | solution.py:69
  (33 shorter events, 1.0 us)
Async XLA Ops:
  6.5 64.9 %all-gather.8.cloned.1.call-start = ((), (), s32[]{:S(2)}) async-start(), calls=%async_computation.3 | async-start | bytes 4325376 | tf_op jit(solution)/shard_map/all_gather | solution.py:30
  8.4 69.2 %copy-start = (bf16[1,16,16,512]{3,2,1,0:T(8,128)(2,1)}, bf16[1,16,16,512]{3,2,1,0:T(8,128)(2,1)S(1)}, u32[]{:S(2)}) copy-start(bf16[1,16,16,512]{3,2,1,0:T(8,128)(2,1)S(1)} %get-tuple-element.13) | copy-start | bytes 786436
  10.0 8.6 %copy-start.3 = (s32[2,16]{1,0:T(2,128)S(1)}, s32[2,16]{1,0:T(2,128)}, u32[]{:S(2)}) copy-start(s32[2,16]{1,0:T(2,128)} %param.13) | copy-start | bytes 388
  10.0 59.8 %all-to-all-start.1 = ((bf16[8,16,16,512]{3,2,1,0:T(8,128)(2,1)}), bf16[8,16,16,512]{3,2,1,0:T(8,128)(2,1)S(1)}, u32[]{:S(2)}, u32[]{:S(2)}) async-start(bf16[8,16,16,512]{3,2,1,0:T(8,128)(2,1)} %broadcast_in_dim.59), calls=%async_computation.1 | async-start | bytes 4194304 | tf_op jit(solution)/shard_map/all_to_all | solution.py:9
  18.6 196.3 %all-gather.16.cloned.1.call-start = ((), (), s32[]{:S(2)}) async-start(), calls=%async_computation.8 | async-start | bytes 9437184 | tf_op jit(solution)/shard_map/all_gather | solution.py:48
  83.2 77.6 %all-to-all-start = ((bf16[8,16,16,512]{3,2,1,0:T(8,128)(2,1)}), bf16[8,16,16,512]{3,2,1,0:T(8,128)(2,1)S(1)}, u32[]{:S(2)}, u32[]{:S(2)}) async-start(bf16[8,16,16,512]{3,2,1,0:T(8,128)(2,1)} %broadcast_in_dim.55), calls=%async_computation | async-start | bytes 4194304 | tf_op jit(solution)/shard_map/all_to_all | solution.py:9
  86.8 223.1 %all-gather.14.cloned.1.call-start = ((), (), s32[]{:S(2)}) async-start(), calls=%async_computation.7 | async-start | bytes 9437184 | tf_op jit(solution)/shard_map/all_gather | solution.py:48
  167.6 4.3 copy-start.1
  171.3 1.0 copy-start.2
  171.3 179.9 %all-gather.12.cloned.1.call-start = ((), (), s32[]{:S(2)}) async-start(), calls=%async_computation.5 | async-start | bytes 2359296 | tf_op jit(solution)/shard_map/all_gather | solution.py:62
  231.9 160.2 %all-gather.10.cloned.1.call-start = ((), (), s32[]{:S(2)}) async-start(), calls=%async_computation.4 | async-start | bytes 2359296 | tf_op jit(solution)/shard_map/all_gather | solution.py:62
  325.8 247.5 %reduce-scatter.2.cloned.1.call-start = ((), (), s32[]{:S(2)}) async-start(), calls=%async_computation.6 | async-start | bytes 8650752 | tf_op jit(solution)/shard_map/reduce_scatter | solution.py:69
Sparse Core Ops, SparseCore 0:
  9.8 56.2 all-gather.7
  81.7 133.1 all-gather.15
  216.7 93.0 all-gather.13
  311.5 39.7 all-gather.11
  352.9 39.1 all-gather.9
  474.7 98.5 reduce-scatter.1
